TPU v7x, 768 devices: a whole 4x8x12 slice. The times are simulated.
768 devices in a mesh: section: 12 (over x, z_hi), dp: 64 (over y, z_lo, core).
Axes of the slice: x: 4, y: 8, z: 12 (z_hi: 3, z_lo: 4; z = z_hi * 4 + z_lo), core: 2. Of those that a mesh axis runs over, the one named last changes fastest.
Arguments:
- buffer: bfloat16 [12, 512, 2048], P('section', 'dp'), may hold values from -6 to 6
- gate_weight: bfloat16 [12, 2, 2048, 8192], P('section', None, None, 'dp'), may hold values from -0.125 to 0.125
- up_weight: bfloat16 [12, 2, 2048, 8192], P('section', None, None, 'dp'), may hold values from -0.125 to 0.125
- down_weight: bfloat16 [12, 2, 8192, 2048], P('section', None, 'dp'), may hold values from -0.09375 to 0.09375
- norm_gain: float32 [12, 2, 2048], P('section'), may hold values from 0.1 to 1.9
- repeat_index: int32 [2, 12], P(None, 'section'), may hold values from 0 to 1
Outputs:
- final_buffer: bfloat16 [12, 512, 2048], P('section', 'dp')
Inputs may be any that keep to these rules, and one draw needn't show every extreme that they name: `repeat_index`: the layer each section applies, one of its 2.
All inputs are finite; a program needn't handle non-finite values.
Results may differ from a plain program's by a relative error of at most 0.01.
Values may be sent and summed in bfloat16 or wider, within the bound.
No kernel may reach another device: no remote copies, remote signals or barrier semaphores. Data moves between devices by JAX's collectives and lax.ppermute only.
A program may use at most 32 MiB of HBM per device.

v0:
```python
import jax
import jax.numpy as jnp
from jax import lax
from jax.experimental import pallas as pl
from jax.experimental.pallas import tpu as pltpu
from jax.sharding import PartitionSpec as P


TICKS = 2
INTERPRET = False


epsilon = 0.5


def passed_along(block, axis, distance):
    devices = range(lax.axis_size(axis))
    route = [((i - distance) % len(devices), i) for i in devices]
    return lax.ppermute(block, axis, route)


def colour(place):
    return (place >> 1 ^ place >> 3) & 1


def same_kind(axis):
    places = sorted(range(lax.axis_size(axis)), key=lambda place: (place & 7, place))
    return [
        [place for place in places if place & 1 == core and colour(place) == shade]
        for core in range(2)
        for shade in range(2)
    ]


def to_other_core(value, axis):
    return lax.ppermute(value, axis, [(place, place ^ 1) for place in range(lax.axis_size(axis))])


def to_other_colour(value, axis, step):
    size = lax.axis_size(axis)
    route = [(place, place ^ 2 if place & 1 else (place + 8 * step) % size) for place in range(size)]
    return lax.ppermute(value, axis, route)


def exchange(blocks, axis, groups):
    return lax.all_to_all(blocks, axis, 0, 0, tiled=True, axis_index_groups=groups)


def room(mebibytes):
    return pltpu.CompilerParams(vmem_limit_bytes=mebibytes << 20)


def spread_kernel(tick, chosen_ref, rows_ref, gain_ref, copies_ref):
    widened = rows_ref[...].astype(jnp.float32)
    squares = jnp.mean(widened * widened, axis=-1, keepdims=True)
    gain_row = gain_ref[pl.ds(chosen_ref[tick], 1), :]
    normed = (widened * lax.rsqrt(squares + epsilon) * gain_row).astype(copies_ref.dtype)
    for member in range(copies_ref.shape[0]):
        copies_ref[member] = normed


def spread(tick, repeat_index, rows, gains, members):
    count, width = rows.shape
    return pl.pallas_call(
        lambda *refs: spread_kernel(tick, *refs),
        out_shape=jax.ShapeDtypeStruct((members, count, width), rows.dtype),
        in_specs=[
            pl.BlockSpec(memory_space=pltpu.SMEM),
            pl.BlockSpec(memory_space=pltpu.VMEM),
            pl.BlockSpec(memory_space=pltpu.VMEM),
        ],
        out_specs=pl.BlockSpec(memory_space=pltpu.VMEM),
        cost_estimate=pl.CostEstimate(flops=8 * count * width, bytes_accessed=2 * members * count * width, transcendentals=8),
        compiler_params=room(4),
        name="spread",
        interpret=INTERPRET,
    )(repeat_index, rows, gains)


def slab_loads(chosen, sources, slabs, arrived):
    return [
        pltpu.make_async_copy(source.at[chosen], slab, arrived.at[index])
        for index, (source, slab) in enumerate(zip(sources, slabs))
    ]


def store_halves(gate_ref, up_ref, down_ref, half_refs):
    width, lanes = gate_ref.shape
    units = lanes // 2
    gate_value = gate_ref[...].astype(jnp.float32)
    up_value = up_ref[...].astype(jnp.float32)
    first = lax.broadcasted_iota(jnp.int32, (width, lanes), 1) < units
    mixed = (
        jnp.where(first, gate_value, pltpu.roll(up_value, units, 1)),
        jnp.where(first, pltpu.roll(gate_value, units, 1), up_value),
    )
    for half, half_ref in enumerate(half_refs):
        half_ref[0:width] = mixed[half].astype(half_ref.dtype)
        for column in range(width // lanes):
            start = width + column * units
            half_ref[start : start + units] = down_ref[
                half * units : (half + 1) * units, column * lanes : (column + 1) * lanes
            ]


def pack_kernel(tick, chosen_ref, gate_hbm, up_hbm, down_hbm, packed_ref, arrived):
    chosen = chosen_ref[tick]
    width, lanes = gate_hbm.shape[1:]
    moves = [
        (gate_hbm.at[chosen], packed_ref.at[0:width]),
        (up_hbm.at[chosen], packed_ref.at[width : 2 * width]),
    ]
    for column in range(width // lanes):
        start = 2 * width + column * lanes
        moves.append(
            (
                down_hbm.at[chosen, :, column * lanes : (column + 1) * lanes],
                packed_ref.at[start : start + lanes],
            )
        )
    copies = [pltpu.make_async_copy(*move, arrived.at[index]) for index, move in enumerate(moves)]
    for copy in copies:
        copy.start()
    for copy in copies:
        copy.wait()


IN_HBM = pl.BlockSpec(memory_space=pltpu.HBM)
IN_VMEM = pl.BlockSpec(memory_space=pltpu.VMEM)
IN_SMEM = pl.BlockSpec(memory_space=pltpu.SMEM)


def halves_of(weight):
    _, width, lanes = weight.shape
    half = jax.ShapeDtypeStruct((width + width // 2, lanes), weight.dtype)
    return half, half


def slabs_of(*weights):
    return [pltpu.VMEM(weight.shape[1:], weight.dtype) for weight in weights]


def pack(tick, chosen, *weights):
    size = weights[0].shape[1] * weights[0].shape[2]
    return pl.pallas_call(
        lambda *refs: pack_kernel(tick, *refs),
        out_shape=jax.ShapeDtypeStruct((3 * weights[0].shape[1], weights[0].shape[2]), weights[0].dtype),
        in_specs=[IN_SMEM, IN_HBM, IN_HBM, IN_HBM],
        out_specs=IN_VMEM,
        scratch_shapes=[pltpu.SemaphoreType.DMA((2 + weights[0].shape[1] // weights[0].shape[2],))],
        cost_estimate=pl.CostEstimate(flops=6 * size, bytes_accessed=12 * size, transcendentals=0),
        compiler_params=room(60),
        name="pack",
        interpret=INTERPRET,
    )(chosen, *weights)


def begin_kernel(
    chosen_ref, rows_hbm, gain_hbm, gate_hbm, up_hbm, down_hbm, first_ref, second_ref, copies_ref, *scratch
):
    slabs, (rows_ref, gain_ref, arrived, loaded) = scratch[:3], scratch[3:]
    early = [
        pltpu.make_async_copy(rows_hbm, rows_ref, loaded.at[0]),
        pltpu.make_async_copy(gain_hbm, gain_ref, loaded.at[1]),
    ]
    for load in early:
        load.start()
    loads = slab_loads(chosen_ref[0], (gate_hbm, up_hbm, down_hbm), slabs, arrived)
    for load in loads:
        load.start()
    for load in early:
        load.wait()
    spread_kernel(0, chosen_ref, rows_ref, gain_ref, copies_ref)
    for load in loads:
        load.wait()
    store_halves(*slabs, (first_ref, second_ref))


def begin(chosen, rows, gains, weights, members):
    size = weights[0].shape[1] * weights[0].shape[2]
    return pl.pallas_call(
        begin_kernel,
        out_shape=(*halves_of(weights[0]), jax.ShapeDtypeStruct((members, *rows.shape), rows.dtype)),
        in_specs=[IN_SMEM] + [IN_HBM] * 5,
        out_specs=(IN_VMEM,) * 3,
        scratch_shapes=slabs_of(*weights)
        + [
            pltpu.VMEM(rows.shape, rows.dtype),
            pltpu.VMEM(gains.shape, gains.dtype),
            pltpu.SemaphoreType.DMA((3,)),
            pltpu.SemaphoreType.DMA((2,)),
        ],
        cost_estimate=pl.CostEstimate(flops=6 * size, bytes_accessed=12 * size, transcendentals=8),
        compiler_params=room(60),
        name="begin",
        interpret=INTERPRET,
    )(chosen, rows, gains, *weights)


def feed_forward_kernel(pieces, tokens_ref, *refs):
    own, refs = refs[:pieces], refs[pieces:]
    count = (len(refs) - 2) // 2
    sources, out_ref, held, arrived = refs[:count], refs[count], refs[count + 1 : -1], refs[-1]
    members, rows, width = tokens_ref.shape
    lanes = own[0].shape[1]
    units = lanes // pieces
    above = 2 * width // pieces
    parts = ((0, above), (above, own[0].shape[0]))
    copies = [
        [
            pltpu.make_async_copy(source.at[start:end], slot.at[start:end], arrived.at[part, index])
            for index, (source, slot) in enumerate(zip(sources, held))
        ]
        for part, (start, end) in enumerate(parts)
    ]
    for part in copies:
        for copy in part:
            copy.start()
    tokens = tokens_ref[...].reshape(members * rows, width)
    everything = (*own, *held)
    first = lax.broadcasted_iota(jnp.int32, (members * rows, lanes), 1) < units
    hidden = []
    for index in range(0, len(everything), pieces):
        shard = everything[index : index + pieces]
        if index:
            for copy in copies[0][index - pieces : index]:
                copy.wait()
        sides = (shard[0][0:width], shard[-1][above - width : above])
        value = jnp.dot(tokens, jnp.concatenate(sides, axis=1), preferred_element_type=jnp.float32)
        gate_value, up_value = value[:, :lanes], value[:, lanes:]
        if pieces == 2:
            left, right = gate_value, up_value
            gate_value = jnp.where(first, left, pltpu.roll(right, units, 1))
            up_value = jnp.where(first, pltpu.roll(left, units, 1), right)
        hidden.append((gate_value / (1.0 + jnp.exp(-gate_value)) * up_value).astype(tokens.dtype))
    hidden = jnp.concatenate(hidden, axis=1)
    for copy in copies[1]:
        copy.wait()
    for column in range(0, width // lanes, 2):
        slabs = []
        for step in range(2):
            start = above + (column + step) * units
            slabs.append(jnp.concatenate([piece[start : start + units] for piece in everything], axis=0))
        value = jnp.dot(hidden, jnp.concatenate(slabs, axis=1), preferred_element_type=jnp.float32)
        out_ref[:, :, column * lanes : (column + 2) * lanes] = value.astype(out_ref.dtype).reshape(
            members, rows, 2 * lanes
        )


def feed_forward(tokens, own, others):
    members, rows, width = tokens.shape
    pieces = len(own)
    weights = sum(piece.size for piece in (*own, *others))
    return pl.pallas_call(
        lambda *refs: feed_forward_kernel(pieces, *refs),
        out_shape=jax.ShapeDtypeStruct(tokens.shape, tokens.dtype),
        in_specs=[IN_VMEM] * (1 + pieces) + [IN_HBM] * len(others),
        out_specs=IN_VMEM,
        scratch_shapes=[pltpu.VMEM(other.shape, other.dtype) for other in others]
        + [pltpu.SemaphoreType.DMA((2, len(others)))],
        cost_estimate=pl.CostEstimate(
            flops=2 * members * rows * weights,
            bytes_accessed=2 * weights,
            transcendentals=members * rows * weights // (3 * width),
        ),
        compiler_params=room(8),
        name="ffn",
        interpret=INTERPRET,
    )(tokens, *own, *others)


def advance_kernel(parts_ref, rows_ref, out_ref):
    total = rows_ref[...].astype(jnp.float32)
    output = parts_ref[0].astype(jnp.float32)
    for member in range(1, parts_ref.shape[0]):
        output = output + parts_ref[member].astype(jnp.float32)
    out_ref[...] = (total + output).astype(out_ref.dtype)


def advance(parts, rows):
    return pl.pallas_call(
        advance_kernel,
        out_shape=jax.ShapeDtypeStruct(rows.shape, rows.dtype),
        in_specs=[pl.BlockSpec(memory_space=pltpu.VMEM)] * 2,
        out_specs=pl.BlockSpec(memory_space=pltpu.VMEM),
        cost_estimate=pl.CostEstimate(flops=parts.size, bytes_accessed=2 * parts.size, transcendentals=0),
        compiler_params=room(4),
        name="advance",
        interpret=INTERPRET,
    )(parts, rows)


def on_device(buffer, gate_weight, up_weight, down_weight, norm_gain, repeat_index):
    current = buffer[0]
    chosen = repeat_index.reshape(TICKS)
    weights = (gate_weight[0], up_weight[0], down_weight[0])
    groups = same_kind("dp")
    members = len(groups[0])
    for tick in range(TICKS):
        if tick == 0:
            *own, copies = begin(chosen, current, norm_gain[0], weights, members)
        else:
            own = [pack(tick, chosen, *weights)]
            copies = spread(tick, chosen, current, norm_gain[0], members)
        near, pair, far = [], [], []
        for index, packed in enumerate(own):
            near.append(to_other_colour(packed, "dp", 1 if tick or index else -1))
            pair.append(to_other_core(packed, "dp"))
            far.append(to_other_core(near[-1], "dp"))
        tokens = exchange(copies, "dp", groups)
        partial_value = feed_forward(tokens, own, (*pair, *near, *far))
        parts = exchange(partial_value, "dp", groups)
        advanced = advance(parts, current)
        current = passed_along(advanced, "section", 1)
    return current[None]


def solution(mesh):
    placed = (
        P("section", "dp", None),
        P("section", None, None, "dp"),
        P("section", None, None, "dp"),
        P("section", None, "dp", None),
        P("section", None, None),
        P(None, "section"),
    )
    return jax.shard_map(
        on_device, mesh=mesh, in_specs=placed, out_specs=P("section", "dp", None), check_vma=False
    )
```

profile of v0, /device:TPU:8, one launch (start us, length us, event | category | flops | bytes accessed | tf_op | source)
XLA Modules:
  0.0 158.4 jit_solution(851089627240107744)
XLA Ops:
  0.0 3.9 %begin.1 = (bf16[3072,128]{1,0:T(8,128)(2,1)}, bf16[3072,128]{1,0:T(8,128)(2,1)}, bf16[16,8,2048]{2,1,0:T(8,128)(2,1)}) custom-call(s32[2]{0:T(128)} %bitcast.11, bf16[8,2048]{1,0:T(8,128)(2,1)} %bitcast.7, f32[2,2048]{1,0:T(2,128)} %bitcast.9, bf16[2,2048,128]{2,1,0:T(8,128)(2,1)} %bitcast.14, bf16[2,2048,128]{2,1,0:T(8,128)(2,1)} %bitcast.16, ...), custom_call_target="tpu_custom_call" | custom-call | flops 1572864 | bytes 3145728 | tf_op jit(solution)/shard_map/begin/pallas_call | solution.py:181
  3.9 11.3 %collective-permute-start.2 = (bf16[3072,128]{1,0:T(8,128)(2,1)}, bf16[3072,128]{1,0:T(8,128)(2,1)}, u32[]{:S(2)}, u32[]{:S(2)}) collective-permute-start(bf16[3072,128]{1,0:T(8,128)(2,1)} %get-tuple-element.9.refs_1_), channel_id=1, source_target_pairs={{0,56},{1,3},{2,58},{3,1},{4,60},{5,7},{6,62},{7,5},{8,0},{9,11},{... | collective-permute-start | bytes 2359304 | tf_op jit(solution)/shard_map/ppermute | solution.py:42
  15.2 1.9 %collective-permute-start.3 = (bf16[3072,128]{1,0:T(8,128)(2,1)}, bf16[3072,128]{1,0:T(8,128)(2,1)}, u32[]{:S(2)}, u32[]{:S(2)}) collective-permute-start(bf16[3072,128]{1,0:T(8,128)(2,1)} %get-tuple-element.10.refs_2_), channel_id=1, source_target_pairs={{0,8},{1,3},{2,10},{3,1},{4,12},{5,7},{6,14},{7,5},{8,16},{9,11},{... | collective-permute-start | bytes 2359304 | tf_op jit(solution)/shard_map/ppermute | solution.py:42
  17.2 4.2 %all-to-all-start = ((bf16[16,8,2048]{2,1,0:T(8,128)(2,1)}), bf16[16,8,2048]{2,1,0:T(8,128)(2,1)S(1)}, u32[]{:S(2)}, u32[]{:S(2)}) async-start(bf16[16,8,2048]{2,1,0:T(8,128)(2,1)} %get-tuple-element.8), calls=%async_computation | async-start | bytes 1048576 | tf_op jit(solution)/shard_map/all_to_all | solution.py:46
  21.4 0.0 copy-start.1
  21.4 2.1 %collective-permute-start = (bf16[3072,128]{1,0:T(8,128)(2,1)}, bf16[3072,128]{1,0:T(8,128)(2,1)}, u32[]{:S(2)}, u32[]{:S(2)}) collective-permute-start(bf16[3072,128]{1,0:T(8,128)(2,1)} %get-tuple-element.9.refs_1_), channel_id=1, source_target_pairs={{0,1},{1,0},{2,3},{3,2},{4,5},{5,4},{6,7},{7,6},{8,9},{9,8},{10,11... | collective-permute-start | bytes 2359304 | tf_op jit(solution)/shard_map/ppermute | solution.py:36
  23.5 2.4 %collective-permute-start.1 = (bf16[3072,128]{1,0:T(8,128)(2,1)}, bf16[3072,128]{1,0:T(8,128)(2,1)}, u32[]{:S(2)}, u32[]{:S(2)}) collective-permute-start(bf16[3072,128]{1,0:T(8,128)(2,1)} %get-tuple-element.10.refs_2_), channel_id=1, source_target_pairs={{0,1},{1,0},{2,3},{3,2},{4,5},{5,4},{6,7},{7,6},{8,9},{9,8},{10,11... | collective-permute-start | bytes 2359304 | tf_op jit(solution)/shard_map/ppermute | solution.py:36
  25.9 9.0 %collective-permute-done.2.refs_5_ = bf16[3072,128]{1,0:T(8,128)(2,1)} collective-permute-done((bf16[3072,128]{1,0:T(8,128)(2,1)}, bf16[3072,128]{1,0:T(8,128)(2,1)}, u32[]{:S(2)}, u32[]{:S(2)}) %collective-permute-start.2) | collective-permute-done | bytes 786464 | tf_op jit(solution)/shard_map/ppermute | solution.py:42
  34.9 1.9 %collective-permute-start.4 = (bf16[3072,128]{1,0:T(8,128)(2,1)}, bf16[3072,128]{1,0:T(8,128)(2,1)}, u32[]{:S(2)}, u32[]{:S(2)}) collective-permute-start(bf16[3072,128]{1,0:T(8,128)(2,1)} %collective-permute-done.2.refs_5_), channel_id=1, source_target_pairs={{0,1},{1,0},{2,3},{3,2},{4,5},{5,4},{6,7},{7,6},{8,9},{9,8},{10,11... | collective-permute-start | bytes 2359304 | tf_op jit(solution)/shard_map/ppermute | solution.py:36
  36.8 2.1 %collective-permute-done.3.refs_6_ = bf16[3072,128]{1,0:T(8,128)(2,1)} collective-permute-done((bf16[3072,128]{1,0:T(8,128)(2,1)}, bf16[3072,128]{1,0:T(8,128)(2,1)}, u32[]{:S(2)}, u32[]{:S(2)}) %collective-permute-start.3) | collective-permute-done | bytes 786464 | tf_op jit(solution)/shard_map/ppermute | solution.py:42
  38.9 1.9 %collective-permute-start.5 = (bf16[3072,128]{1,0:T(8,128)(2,1)}, bf16[3072,128]{1,0:T(8,128)(2,1)}, u32[]{:S(2)}, u32[]{:S(2)}) collective-permute-start(bf16[3072,128]{1,0:T(8,128)(2,1)} %collective-permute-done.3.refs_6_), channel_id=1, source_target_pairs={{0,1},{1,0},{2,3},{3,2},{4,5},{5,4},{6,7},{7,6},{8,9},{9,8},{10,11... | collective-permute-start | bytes 2359304 | tf_op jit(solution)/shard_map/ppermute | solution.py:36
  40.8 0.0 copy-start.3
  40.8 3.4 %pack.1.refs_1_ = bf16[6144,128]{1,0:T(8,128)(2,1)} custom-call(s32[2]{0:T(128)} %bitcast.12, bf16[2,2048,128]{2,1,0:T(8,128)(2,1)} %bitcast.15, bf16[2,2048,128]{2,1,0:T(8,128)(2,1)} %bitcast.17, bf16[2,128,2048]{2,1,0:T(8,128)(2,1)} %bitcast.19), custom_call_target="tpu_custom_call" | custom-call | flops 1572864 | bytes 3145728 | tf_op jit(solution)/shard_map/pack/pallas_call | solution.py:145
  44.2 0.0 copy-start
  44.2 2.1 %collective-permute-start.8 = (bf16[6144,128]{1,0:T(8,128)(2,1)}, bf16[6144,128]{1,0:T(8,128)(2,1)}, u32[]{:S(2)}, u32[]{:S(2)}) collective-permute-start(bf16[6144,128]{1,0:T(8,128)(2,1)} %pack.1.refs_1_), channel_id=1, source_target_pairs={{0,8},{1,3},{2,10},{3,1},{4,12},{5,7},{6,14},{7,5},{8,16},{9,11},{... | collective-permute-start | bytes 4718600 | tf_op jit(solution)/shard_map/ppermute | solution.py:42
  46.3 0.0 collective-permute-done.refs_3_
  46.3 0.0 collective-permute-done.1.refs_4_
  46.3 0.0 all-to-all-done.refs_0_
  46.3 0.0 collective-permute-done.4.refs_7_
  46.3 0.0 collective-permute-done.5.refs_8_
  46.3 0.0 copy-done.1
  46.3 0.0 copy-start.2
  46.4 1.1 copy-done.2
  47.5 4.4 %ffn.2 = bf16[16,8,2048]{2,1,0:T(8,128)(2,1)} custom-call(bf16[16,8,2048]{2,1,0:T(8,128)(2,1)S(1)} %all-to-all-done.refs_0_, bf16[3072,128]{1,0:T(8,128)(2,1)S(1)} %copy-done.1, bf16[3072,128]{1,0:T(8,128)(2,1)S(1)} %copy-done.2, bf16[3072,128]{1,0:T(8,128)(2,1)} %collective-permute-done.refs_3_, bf16[3072,128]{1,0:T(8,128)(2,1)} %collective-permute-done.1.refs_4_, ...), custom_call_target="tpu_custom_call" | custom-call | flops 805306368 | bytes 6291456 | tf_op jit(solution)/shard_map/ffn/pallas_call | solution.py:254
  51.9 0.0 copy-start.4
  51.9 0.0 copy-start.5
  51.9 6.0 %all-to-all-start.1 = ((bf16[16,8,2048]{2,1,0:T(8,128)(2,1)}), bf16[16,8,2048]{2,1,0:T(8,128)(2,1)S(1)}, u32[]{:S(2)}, u32[]{:S(2)}) async-start(bf16[16,8,2048]{2,1,0:T(8,128)(2,1)} %ffn.2), calls=%async_computation.1 | async-start | bytes 1048576 | tf_op jit(solution)/shard_map/all_to_all | solution.py:46
  57.9 0.0 copy-done
  57.9 1.9 %collective-permute-start.7 = (bf16[6144,128]{1,0:T(8,128)(2,1)S(1)}, bf16[6144,128]{1,0:T(8,128)(2,1)}, u32[]{:S(2)}, u32[]{:S(2)}) collective-permute-start(bf16[6144,128]{1,0:T(8,128)(2,1)S(1)} %copy-done), channel_id=1, source_target_pairs={{0,1},{1,0},{2,3},{3,2},{4,5},{5,4},{6,7},{7,6},{8,9},{9,8},{10,11... | collective-permute-start | bytes 4718600 | tf_op jit(solution)/shard_map/ppermute | solution.py:36
  59.8 17.0 %collective-permute-done.8.refs_3_ = bf16[6144,128]{1,0:T(8,128)(2,1)} collective-permute-done((bf16[6144,128]{1,0:T(8,128)(2,1)}, bf16[6144,128]{1,0:T(8,128)(2,1)}, u32[]{:S(2)}, u32[]{:S(2)}) %collective-permute-start.8) | collective-permute-done | bytes 1572896 | tf_op jit(solution)/shard_map/ppermute | solution.py:42
  76.8 1.9 %collective-permute-start.9 = (bf16[6144,128]{1,0:T(8,128)(2,1)}, bf16[6144,128]{1,0:T(8,128)(2,1)}, u32[]{:S(2)}, u32[]{:S(2)}) collective-permute-start(bf16[6144,128]{1,0:T(8,128)(2,1)} %collective-permute-done.8.refs_3_), channel_id=1, source_target_pairs={{0,1},{1,0},{2,3},{3,2},{4,5},{5,4},{6,7},{7,6},{8,9},{9,8},{10,11... | collective-permute-start | bytes 4718600 | tf_op jit(solution)/shard_map/ppermute | solution.py:36
  78.7 2.0 %all-to-all-done.1.parts_ref = bf16[16,8,2048]{2,1,0:T(8,128)(2,1)S(1)} async-done(((bf16[16,8,2048]{2,1,0:T(8,128)(2,1)}), bf16[16,8,2048]{2,1,0:T(8,128)(2,1)S(1)}, u32[]{:S(2)}, u32[]{:S(2)}) %all-to-all-start.1) | async-done | bytes 524320 | tf_op jit(solution)/shard_map/all_to_all | solution.py:46
  80.7 0.0 copy-done.3
  80.7 0.1 advance.2
  80.8 5.3 %collective-permute-start.6 = (bf16[8,2048]{1,0:T(8,128)(2,1)S(1)}, bf16[8,2048]{1,0:T(8,128)(2,1)S(1)}, u32[]{:S(2)}, u32[]{:S(2)}) collective-permute-start(bf16[8,2048]{1,0:T(8,128)(2,1)S(1)} %advance.2), channel_id=1, source_target_pairs={{704,0},{0,64},{64,128},{128,192},{192,256},{256,320},{320,384},{3... | collective-permute-start | bytes 98312 | tf_op jit(solution)/shard_map/ppermute | solution.py:19
  86.0 7.0 %collective-permute-done.6.refs_1_.rows_ref = bf16[8,2048]{1,0:T(8,128)(2,1)S(1)} collective-permute-done((bf16[8,2048]{1,0:T(8,128)(2,1)S(1)}, bf16[8,2048]{1,0:T(8,128)(2,1)S(1)}, u32[]{:S(2)}, u32[]{:S(2)}) %collective-permute-start.6) | collective-permute-done | bytes 32800 | tf_op jit(solution)/shard_map/ppermute | solution.py:19
  93.0 0.0 copy-done.4
  93.0 1.5 spread.1
  94.5 8.9 %all-to-all-start.2 = ((bf16[16,8,2048]{2,1,0:T(8,128)(2,1)}), bf16[16,8,2048]{2,1,0:T(8,128)(2,1)S(1)}, u32[]{:S(2)}, u32[]{:S(2)}) async-start(bf16[16,8,2048]{2,1,0:T(8,128)(2,1)} %spread.1), calls=%async_computation.2 | async-start | bytes 1048576 | tf_op jit(solution)/shard_map/all_to_all | solution.py:46
  103.4 0.0 collective-permute-done.7.refs_2_
  103.4 0.0 collective-permute-done.9.refs_4_
  103.4 17.1 %all-to-all-done.2.refs_0_ = bf16[16,8,2048]{2,1,0:T(8,128)(2,1)S(1)} async-done(((bf16[16,8,2048]{2,1,0:T(8,128)(2,1)}), bf16[16,8,2048]{2,1,0:T(8,128)(2,1)S(1)}, u32[]{:S(2)}, u32[]{:S(2)}) %all-to-all-start.2) | async-done | bytes 524320 | tf_op jit(solution)/shard_map/all_to_all | solution.py:46
  120.5 3.0 %ffn.3 = bf16[16,8,2048]{2,1,0:T(8,128)(2,1)S(1)} custom-call(bf16[16,8,2048]{2,1,0:T(8,128)(2,1)S(1)} %all-to-all-done.2.refs_0_, bf16[6144,128]{1,0:T(8,128)(2,1)S(1)} %copy-done, bf16[6144,128]{1,0:T(8,128)(2,1)} %collective-permute-done.7.refs_2_, bf16[6144,128]{1,0:T(8,128)(2,1)} %collective-permute-done.8.refs_3_, ...), custom_call_target="tpu_custom_call" | custom-call | flops 805306368 | bytes 6291456 | tf_op jit(solution)/shard_map/ffn/pallas_call | solution.py:254
  123.6 21.7 %all_to_all.20.parts_ref = bf16[16,8,2048]{2,1,0:T(8,128)(2,1)S(1)} all-to-all(bf16[16,8,2048]{2,1,0:T(8,128)(2,1)S(1)} %ffn.3), channel_id=1, replica_groups={{0,16,32,48,10,26,42,58,4,20,36,52,14,30,46,62},{8,24,40,56,2,18,34,50,..., dimensions={0} | all-to-all | bytes 1048576 | tf_op jit(solution)/shard_map/all_to_all | solution.py:46
  145.3 0.1 advance.3
  145.4 3.0 %collective-permute-start.10 = (bf16[8,2048]{1,0:T(8,128)(2,1)S(1)}, bf16[8,2048]{1,0:T(8,128)(2,1)S(1)}, u32[]{:S(2)}, u32[]{:S(2)}) collective-permute-start(bf16[8,2048]{1,0:T(8,128)(2,1)S(1)} %advance.3), channel_id=1, source_target_pairs={{704,0},{0,64},{64,128},{128,192},{192,256},{256,320},{320,384},{3... | collective-permute-start | bytes 98312 | tf_op jit(solution)/shard_map/ppermute | solution.py:19
  148.4 9.4 %collective-permute-done.10 = bf16[8,2048]{1,0:T(8,128)(2,1)S(1)} collective-permute-done((bf16[8,2048]{1,0:T(8,128)(2,1)S(1)}, bf16[8,2048]{1,0:T(8,128)(2,1)S(1)}, u32[]{:S(2)}, u32[]{:S(2)}) %collective-permute-start.10) | collective-permute-done | bytes 32800 | tf_op jit(solution)/shard_map/ppermute | solution.py:19
  157.8 0.6 copy.8
  (1 shorter events, 0.0 us)
Async XLA Ops:
  3.9 31.0 %collective-permute-start.2 = (bf16[3072,128]{1,0:T(8,128)(2,1)}, bf16[3072,128]{1,0:T(8,128)(2,1)}, u32[]{:S(2)}, u32[]{:S(2)}) collective-permute-start(bf16[3072,128]{1,0:T(8,128)(2,1)} %get-tuple-element.9.refs_1_), channel_id=1, source_target_pairs={{0,56},{1,3},{2,58},{3,1},{4,60},{5,7},{6,62},{7,5},{8,0},{9,11},{... | collective-permute-start | bytes 2359304 | tf_op jit(solution)/shard_map/ppermute | solution.py:42
  15.2 23.7 %collective-permute-start.3 = (bf16[3072,128]{1,0:T(8,128)(2,1)}, bf16[3072,128]{1,0:T(8,128)(2,1)}, u32[]{:S(2)}, u32[]{:S(2)}) collective-permute-start(bf16[3072,128]{1,0:T(8,128)(2,1)} %get-tuple-element.10.refs_2_), channel_id=1, source_target_pairs={{0,8},{1,3},{2,10},{3,1},{4,12},{5,7},{6,14},{7,5},{8,16},{9,11},{... | collective-permute-start | bytes 2359304 | tf_op jit(solution)/shard_map/ppermute | solution.py:42
  17.2 29.1 %all-to-all-start = ((bf16[16,8,2048]{2,1,0:T(8,128)(2,1)}), bf16[16,8,2048]{2,1,0:T(8,128)(2,1)S(1)}, u32[]{:S(2)}, u32[]{:S(2)}) async-start(bf16[16,8,2048]{2,1,0:T(8,128)(2,1)} %get-tuple-element.8), calls=%async_computation | async-start | bytes 1048576 | tf_op jit(solution)/shard_map/all_to_all | solution.py:46
  21.4 25.0 %copy-start.1 = (bf16[3072,128]{1,0:T(8,128)(2,1)S(1)}, bf16[3072,128]{1,0:T(8,128)(2,1)}, u32[]{:S(2)}) copy-start(bf16[3072,128]{1,0:T(8,128)(2,1)} %get-tuple-element.9.refs_1_) | copy-start | bytes 2359300
  21.4 24.9 %collective-permute-start = (bf16[3072,128]{1,0:T(8,128)(2,1)}, bf16[3072,128]{1,0:T(8,128)(2,1)}, u32[]{:S(2)}, u32[]{:S(2)}) collective-permute-start(bf16[3072,128]{1,0:T(8,128)(2,1)} %get-tuple-element.9.refs_1_), channel_id=1, source_target_pairs={{0,1},{1,0},{2,3},{3,2},{4,5},{5,4},{6,7},{7,6},{8,9},{9,8},{10,11... | collective-permute-start | bytes 2359304 | tf_op jit(solution)/shard_map/ppermute | solution.py:36
  23.5 22.8 %collective-permute-start.1 = (bf16[3072,128]{1,0:T(8,128)(2,1)}, bf16[3072,128]{1,0:T(8,128)(2,1)}, u32[]{:S(2)}, u32[]{:S(2)}) collective-permute-start(bf16[3072,128]{1,0:T(8,128)(2,1)} %get-tuple-element.10.refs_2_), channel_id=1, source_target_pairs={{0,1},{1,0},{2,3},{3,2},{4,5},{5,4},{6,7},{7,6},{8,9},{9,8},{10,11... | collective-permute-start | bytes 2359304 | tf_op jit(solution)/shard_map/ppermute | solution.py:36
  34.9 11.4 %collective-permute-start.4 = (bf16[3072,128]{1,0:T(8,128)(2,1)}, bf16[3072,128]{1,0:T(8,128)(2,1)}, u32[]{:S(2)}, u32[]{:S(2)}) collective-permute-start(bf16[3072,128]{1,0:T(8,128)(2,1)} %collective-permute-done.2.refs_5_), channel_id=1, source_target_pairs={{0,1},{1,0},{2,3},{3,2},{4,5},{5,4},{6,7},{7,6},{8,9},{9,8},{10,11... | collective-permute-start | bytes 2359304 | tf_op jit(solution)/shard_map/ppermute | solution.py:36
  38.9 7.4 %collective-permute-start.5 = (bf16[3072,128]{1,0:T(8,128)(2,1)}, bf16[3072,128]{1,0:T(8,128)(2,1)}, u32[]{:S(2)}, u32[]{:S(2)}) collective-permute-start(bf16[3072,128]{1,0:T(8,128)(2,1)} %collective-permute-done.3.refs_6_), channel_id=1, source_target_pairs={{0,1},{1,0},{2,3},{3,2},{4,5},{5,4},{6,7},{7,6},{8,9},{9,8},{10,11... | collective-permute-start | bytes 2359304 | tf_op jit(solution)/shard_map/ppermute | solution.py:36
  40.8 39.9 %copy-start.3 = (bf16[1,8,2048]{2,1,0:T(8,128)(2,1)S(1)}, bf16[1,8,2048]{2,1,0:T(8,128)(2,1)}, u32[]{:S(2)}) copy-start(bf16[1,8,2048]{2,1,0:T(8,128)(2,1)} %param.6) | copy-start | bytes 98308
  44.2 13.7 %copy-start = (bf16[6144,128]{1,0:T(8,128)(2,1)S(1)}, bf16[6144,128]{1,0:T(8,128)(2,1)}, u32[]{:S(2)}) copy-start(bf16[6144,128]{1,0:T(8,128)(2,1)} %pack.1.refs_1_) | copy-start | bytes 4718596
  44.2 32.6 %collective-permute-start.8 = (bf16[6144,128]{1,0:T(8,128)(2,1)}, bf16[6144,128]{1,0:T(8,128)(2,1)}, u32[]{:S(2)}, u32[]{:S(2)}) collective-permute-start(bf16[6144,128]{1,0:T(8,128)(2,1)} %pack.1.refs_1_), channel_id=1, source_target_pairs={{0,8},{1,3},{2,10},{3,1},{4,12},{5,7},{6,14},{7,5},{8,16},{9,11},{... | collective-permute-start | bytes 4718600 | tf_op jit(solution)/shard_map/ppermute | solution.py:42
  46.3 1.1 copy-start.2
  51.9 41.1 %copy-start.4 = (f32[1,2,2048]{2,1,0:T(2,128)S(1)}, f32[1,2,2048]{2,1,0:T(2,128)}, u32[]{:S(2)}) copy-start(f32[1,2,2048]{2,1,0:T(2,128)} %param.10) | copy-start | bytes 49156
  51.9 41.1 %copy-start.5 = (s32[2,1]{0,1:T(1,128)S(1)}, s32[2,1]{0,1:T(1,128)}, u32[]{:S(2)}) copy-start(s32[2,1]{0,1:T(1,128)} %param.11) | copy-start | bytes 28
  51.9 28.8 %all-to-all-start.1 = ((bf16[16,8,2048]{2,1,0:T(8,128)(2,1)}), bf16[16,8,2048]{2,1,0:T(8,128)(2,1)S(1)}, u32[]{:S(2)}, u32[]{:S(2)}) async-start(bf16[16,8,2048]{2,1,0:T(8,128)(2,1)} %ffn.2), calls=%async_computation.1 | async-start | bytes 1048576 | tf_op jit(solution)/shard_map/all_to_all | solution.py:46
  57.9 45.5 %collective-permute-start.7 = (bf16[6144,128]{1,0:T(8,128)(2,1)S(1)}, bf16[6144,128]{1,0:T(8,128)(2,1)}, u32[]{:S(2)}, u32[]{:S(2)}) collective-permute-start(bf16[6144,128]{1,0:T(8,128)(2,1)S(1)} %copy-done), channel_id=1, source_target_pairs={{0,1},{1,0},{2,3},{3,2},{4,5},{5,4},{6,7},{7,6},{8,9},{9,8},{10,11... | collective-permute-start | bytes 4718600 | tf_op jit(solution)/shard_map/ppermute | solution.py:36
  76.8 26.6 %collective-permute-start.9 = (bf16[6144,128]{1,0:T(8,128)(2,1)}, bf16[6144,128]{1,0:T(8,128)(2,1)}, u32[]{:S(2)}, u32[]{:S(2)}) collective-permute-start(bf16[6144,128]{1,0:T(8,128)(2,1)} %collective-permute-done.8.refs_3_), channel_id=1, source_target_pairs={{0,1},{1,0},{2,3},{3,2},{4,5},{5,4},{6,7},{7,6},{8,9},{9,8},{10,11... | collective-permute-start | bytes 4718600 | tf_op jit(solution)/shard_map/ppermute | solution.py:36
  80.8 12.3 %collective-permute-start.6 = (bf16[8,2048]{1,0:T(8,128)(2,1)S(1)}, bf16[8,2048]{1,0:T(8,128)(2,1)S(1)}, u32[]{:S(2)}, u32[]{:S(2)}) collective-permute-start(bf16[8,2048]{1,0:T(8,128)(2,1)S(1)} %advance.2), channel_id=1, source_target_pairs={{704,0},{0,64},{64,128},{128,192},{192,256},{256,320},{320,384},{3... | collective-permute-start | bytes 98312 | tf_op jit(solution)/shard_map/ppermute | solution.py:19
  94.5 26.0 %all-to-all-start.2 = ((bf16[16,8,2048]{2,1,0:T(8,128)(2,1)}), bf16[16,8,2048]{2,1,0:T(8,128)(2,1)S(1)}, u32[]{:S(2)}, u32[]{:S(2)}) async-start(bf16[16,8,2048]{2,1,0:T(8,128)(2,1)} %spread.1), calls=%async_computation.2 | async-start | bytes 1048576 | tf_op jit(solution)/shard_map/all_to_all | solution.py:46
  145.4 12.4 %collective-permute-start.10 = (bf16[8,2048]{1,0:T(8,128)(2,1)S(1)}, bf16[8,2048]{1,0:T(8,128)(2,1)S(1)}, u32[]{:S(2)}, u32[]{:S(2)}) collective-permute-start(bf16[8,2048]{1,0:T(8,128)(2,1)S(1)} %advance.3), channel_id=1, source_target_pairs={{704,0},{0,64},{64,128},{128,192},{192,256},{256,320},{320,384},{3... | collective-permute-start | bytes 98312 | tf_op jit(solution)/shard_map/ppermute | solution.py:19
where the time goes:
time: 159 us; the launch traced here: 158 us
  waiting for transfers between devices  63.6 us (40%)
  starting transfers between devices  54.8 us (34%)
  blocking collectives  21.7 us (14%)
  Pallas kernels  16.3 us (10%)
  local copies, waits for them, and re-layouts  1.77 us (1%)
    ppermute x3, waiting for transfers between devices, to_other_colour(): return lax.ppermute(value, axis, route)  28.1 us
    all_to_all x1, blocking collectives, exchange(): lax.all_to_all(blocks, axis, 0, 0, tiled=True, axis_index_groups=groups)  21.7 us
    all_to_all x3, waiting for transfers between devices, exchange(): lax.all_to_all(blocks, axis, 0, 0, tiled=True, axis_index_groups=groups)  19.1 us
    all_to_all x3, starting transfers between devices, exchange(): lax.all_to_all(blocks, axis, 0, 0, tiled=True, axis_index_groups=groups)  19.1 us
    ppermute x2, waiting for transfers between devices, passed_along(): return lax.ppermute(block, axis, route)  16.4 us
    ppermute x3, starting transfers between devices, to_other_colour(): return lax.ppermute(value, axis, route)  15.3 us
    ppermute x6, starting transfers between devices, to_other_core(): lax.ppermute(value, axis, [(place, place ^ 1) for place in range(lax.axis...  12.1 us
    ppermute x2, starting transfers between devices, passed_along(): return lax.ppermute(block, axis, route)  8.3 us
  transfers between devices with their start and end apart: 14, of which 7 were waited for; matrix products, arithmetic and copies ran while one was open for 0% of the time, Pallas kernels for 6%

commit v1 on v0

--- a/solution.py
+++ b/solution.py
@@ -197,15 +197,17 @@
     )(chosen, rows, gains, *weights)
 
 
-def feed_forward_kernel(pieces, tokens_ref, *refs):
-    own, refs = refs[:pieces], refs[pieces:]
-    count = (len(refs) - 2) // 2
-    sources, out_ref, held, arrived = refs[:count], refs[count], refs[count + 1 : -1], refs[-1]
+def feed_forward_kernel(pieces, near_by, tokens_ref, *refs):
+    resident, refs = refs[:near_by], refs[near_by:]
+    count = (len(refs) - 1) // 2
+    sources, out_ref, held, arrived = refs[:count], refs[count], refs[count + 1 : 2 * count + 1], refs[-1]
     members, rows, width = tokens_ref.shape
-    lanes = own[0].shape[1]
+    lanes = resident[0].shape[1]
     units = lanes // pieces
     above = 2 * width // pieces
-    parts = ((0, above), (above, own[0].shape[0]))
+    size = 3 * width // pieces
+    own = [ref.at[start : start + size] for ref in resident for start in range(0, ref.shape[0], size)]
+    parts = ((0, above), (above, size))
     copies = [
         [
             pltpu.make_async_copy(source.at[start:end], slot.at[start:end], arrived.at[part, index])
@@ -222,8 +224,8 @@
     hidden = []
     for index in range(0, len(everything), pieces):
         shard = everything[index : index + pieces]
-        if index:
-            for copy in copies[0][index - pieces : index]:
+        if index >= len(own):
+            for copy in copies[0][index - len(own) : index - len(own) + pieces]:
                 copy.wait()
         sides = (shard[0][0:width], shard[-1][above - width : above])
         value = jnp.dot(tokens, jnp.concatenate(sides, axis=1), preferred_element_type=jnp.float32)
@@ -247,17 +249,16 @@
         )
 
 
-def feed_forward(tokens, own, others):
+def feed_forward(tokens, pieces, resident, others):
     members, rows, width = tokens.shape
-    pieces = len(own)
-    weights = sum(piece.size for piece in (*own, *others))
-    return pl.pallas_call(
-        lambda *refs: feed_forward_kernel(pieces, *refs),
+    weights = sum(piece.size for piece in (*resident, *others))
+    arrived = [pltpu.SemaphoreType.DMA((2, len(others)))] if others else []
+    return pl.pallas_call(
+        lambda *refs: feed_forward_kernel(pieces, len(resident), *refs),
         out_shape=jax.ShapeDtypeStruct(tokens.shape, tokens.dtype),
-        in_specs=[IN_VMEM] * (1 + pieces) + [IN_HBM] * len(others),
+        in_specs=[IN_VMEM] * (1 + len(resident)) + [IN_HBM] * len(others),
         out_specs=IN_VMEM,
-        scratch_shapes=[pltpu.VMEM(other.shape, other.dtype) for other in others]
-        + [pltpu.SemaphoreType.DMA((2, len(others)))],
+        scratch_shapes=[pltpu.VMEM(other.shape, other.dtype) for other in others] + arrived,
         cost_estimate=pl.CostEstimate(
             flops=2 * members * rows * weights,
             bytes_accessed=2 * weights,
@@ -266,7 +267,7 @@
         compiler_params=room(8),
         name="ffn",
         interpret=INTERPRET,
-    )(tokens, *own, *others)
+    )(tokens, *resident, *others)
 
 
 def advance_kernel(parts_ref, rows_ref, out_ref):
@@ -308,7 +309,9 @@
             pair.append(to_other_core(packed, "dp"))
             far.append(to_other_core(near[-1], "dp"))
         tokens = exchange(copies, "dp", groups)
-        partial_value = feed_forward(tokens, own, (*pair, *near, *far))
+        others = (*pair, *near, *far)
+        resident, streamed = ((*own, *others), ()) if tick else (own, others)
+        partial_value = feed_forward(tokens, len(own), resident, streamed)
         parts = exchange(partial_value, "dp", groups)
         advanced = advance(parts, current)
         current = passed_along(advanced, "section", 1)

time: 159 us -> 160 us (level)
  no operation moved by 1% of the time
where the time goes in v1:
time: 160 us; the launch traced here: 159 us
  waiting for transfers between devices  63.6 us (40%)
  starting transfers between devices  54.8 us (34%)
  blocking collectives  21.7 us (14%)
  Pallas kernels  16.7 us (10%)
  local copies, waits for them, and re-layouts  1.77 us (1%)
    ppermute x3, waiting for transfers between devices, to_other_colour(): return lax.ppermute(value, axis, route)  28.1 us
    all_to_all x1, blocking collectives, exchange(): lax.all_to_all(blocks, axis, 0, 0, tiled=True, axis_index_groups=groups)  21.7 us
    all_to_all x3, waiting for transfers between devices, exchange(): lax.all_to_all(blocks, axis, 0, 0, tiled=True, axis_index_groups=groups)  19.1 us
    all_to_all x3, starting transfers between devices, exchange(): lax.all_to_all(blocks, axis, 0, 0, tiled=True, axis_index_groups=groups)  19.1 us
    ppermute x2, waiting for transfers between devices, passed_along(): return lax.ppermute(block, axis, route)  16.4 us
    ppermute x3, starting transfers between devices, to_other_colour(): return lax.ppermute(value, axis, route)  15.3 us
    ppermute x6, starting transfers between devices, to_other_core(): lax.ppermute(value, axis, [(place, place ^ 1) for place in range(lax.axis...  12.1 us
    ppermute x2, starting transfers between devices, passed_along(): return lax.ppermute(block, axis, route)  8.29 us
  transfers between devices with their start and end apart: 14, of which 7 were waited for; matrix products, arithmetic and copies ran while one was open for 0% of the time, Pallas kernels for 6%

profile of v1, /device:TPU:8, one launch (start us, length us, event | category | flops | bytes accessed | tf_op | source)
XLA Modules:
  0.0 158.8 jit_solution(6801361043930981138)
XLA Ops:
  0.0 3.9 %begin.1 = (bf16[3072,128]{1,0:T(8,128)(2,1)}, bf16[3072,128]{1,0:T(8,128)(2,1)}, bf16[16,8,2048]{2,1,0:T(8,128)(2,1)}) custom-call(s32[2]{0:T(128)} %bitcast.11, bf16[8,2048]{1,0:T(8,128)(2,1)} %bitcast.7, f32[2,2048]{1,0:T(2,128)} %bitcast.9, bf16[2,2048,128]{2,1,0:T(8,128)(2,1)} %bitcast.14, bf16[2,2048,128]{2,1,0:T(8,128)(2,1)} %bitcast.16, ...), custom_call_target="tpu_custom_call" | custom-call | flops 1572864 | bytes 3145728 | tf_op jit(solution)/shard_map/begin/pallas_call | solution.py:181
  3.9 11.3 %collective-permute-start.2 = (bf16[3072,128]{1,0:T(8,128)(2,1)}, bf16[3072,128]{1,0:T(8,128)(2,1)}, u32[]{:S(2)}, u32[]{:S(2)}) collective-permute-start(bf16[3072,128]{1,0:T(8,128)(2,1)} %get-tuple-element.9.refs_1_), channel_id=1, source_target_pairs={{0,56},{1,3},{2,58},{3,1},{4,60},{5,7},{6,62},{7,5},{8,0},{9,11},{... | collective-permute-start | bytes 2359304 | tf_op jit(solution)/shard_map/ppermute | solution.py:42
  15.2 1.9 %collective-permute-start.3 = (bf16[3072,128]{1,0:T(8,128)(2,1)}, bf16[3072,128]{1,0:T(8,128)(2,1)}, u32[]{:S(2)}, u32[]{:S(2)}) collective-permute-start(bf16[3072,128]{1,0:T(8,128)(2,1)} %get-tuple-element.10.refs_2_), channel_id=1, source_target_pairs={{0,8},{1,3},{2,10},{3,1},{4,12},{5,7},{6,14},{7,5},{8,16},{9,11},{... | collective-permute-start | bytes 2359304 | tf_op jit(solution)/shard_map/ppermute | solution.py:42
  17.2 4.2 %all-to-all-start = ((bf16[16,8,2048]{2,1,0:T(8,128)(2,1)}), bf16[16,8,2048]{2,1,0:T(8,128)(2,1)S(1)}, u32[]{:S(2)}, u32[]{:S(2)}) async-start(bf16[16,8,2048]{2,1,0:T(8,128)(2,1)} %get-tuple-element.8), calls=%async_computation | async-start | bytes 1048576 | tf_op jit(solution)/shard_map/all_to_all | solution.py:46
  21.4 0.0 copy-start.1
  21.4 2.1 %collective-permute-start = (bf16[3072,128]{1,0:T(8,128)(2,1)}, bf16[3072,128]{1,0:T(8,128)(2,1)}, u32[]{:S(2)}, u32[]{:S(2)}) collective-permute-start(bf16[3072,128]{1,0:T(8,128)(2,1)} %get-tuple-element.9.refs_1_), channel_id=1, source_target_pairs={{0,1},{1,0},{2,3},{3,2},{4,5},{5,4},{6,7},{7,6},{8,9},{9,8},{10,11... | collective-permute-start | bytes 2359304 | tf_op jit(solution)/shard_map/ppermute | solution.py:36
  23.5 2.4 %collective-permute-start.1 = (bf16[3072,128]{1,0:T(8,128)(2,1)}, bf16[3072,128]{1,0:T(8,128)(2,1)}, u32[]{:S(2)}, u32[]{:S(2)}) collective-permute-start(bf16[3072,128]{1,0:T(8,128)(2,1)} %get-tuple-element.10.refs_2_), channel_id=1, source_target_pairs={{0,1},{1,0},{2,3},{3,2},{4,5},{5,4},{6,7},{7,6},{8,9},{9,8},{10,11... | collective-permute-start | bytes 2359304 | tf_op jit(solution)/shard_map/ppermute | solution.py:36
  25.9 9.0 %collective-permute-done.2.refs_5_ = bf16[3072,128]{1,0:T(8,128)(2,1)} collective-permute-done((bf16[3072,128]{1,0:T(8,128)(2,1)}, bf16[3072,128]{1,0:T(8,128)(2,1)}, u32[]{:S(2)}, u32[]{:S(2)}) %collective-permute-start.2) | collective-permute-done | bytes 786464 | tf_op jit(solution)/shard_map/ppermute | solution.py:42
  34.9 1.9 %collective-permute-start.4 = (bf16[3072,128]{1,0:T(8,128)(2,1)}, bf16[3072,128]{1,0:T(8,128)(2,1)}, u32[]{:S(2)}, u32[]{:S(2)}) collective-permute-start(bf16[3072,128]{1,0:T(8,128)(2,1)} %collective-permute-done.2.refs_5_), channel_id=1, source_target_pairs={{0,1},{1,0},{2,3},{3,2},{4,5},{5,4},{6,7},{7,6},{8,9},{9,8},{10,11... | collective-permute-start | bytes 2359304 | tf_op jit(solution)/shard_map/ppermute | solution.py:36
  36.8 2.1 %collective-permute-done.3.refs_6_ = bf16[3072,128]{1,0:T(8,128)(2,1)} collective-permute-done((bf16[3072,128]{1,0:T(8,128)(2,1)}, bf16[3072,128]{1,0:T(8,128)(2,1)}, u32[]{:S(2)}, u32[]{:S(2)}) %collective-permute-start.3) | collective-permute-done | bytes 786464 | tf_op jit(solution)/shard_map/ppermute | solution.py:42
  38.9 1.9 %collective-permute-start.5 = (bf16[3072,128]{1,0:T(8,128)(2,1)}, bf16[3072,128]{1,0:T(8,128)(2,1)}, u32[]{:S(2)}, u32[]{:S(2)}) collective-permute-start(bf16[3072,128]{1,0:T(8,128)(2,1)} %collective-permute-done.3.refs_6_), channel_id=1, source_target_pairs={{0,1},{1,0},{2,3},{3,2},{4,5},{5,4},{6,7},{7,6},{8,9},{9,8},{10,11... | collective-permute-start | bytes 2359304 | tf_op jit(solution)/shard_map/ppermute | solution.py:36
  40.8 0.0 copy-start.3
  40.8 3.4 %pack.1.refs_1_ = bf16[6144,128]{1,0:T(8,128)(2,1)} custom-call(s32[2]{0:T(128)} %bitcast.12, bf16[2,2048,128]{2,1,0:T(8,128)(2,1)} %bitcast.15, bf16[2,2048,128]{2,1,0:T(8,128)(2,1)} %bitcast.17, bf16[2,128,2048]{2,1,0:T(8,128)(2,1)} %bitcast.19), custom_call_target="tpu_custom_call" | custom-call | flops 1572864 | bytes 3145728 | tf_op jit(solution)/shard_map/pack/pallas_call | solution.py:145
  44.2 0.0 copy-start
  44.2 2.1 %collective-permute-start.8 = (bf16[6144,128]{1,0:T(8,128)(2,1)}, bf16[6144,128]{1,0:T(8,128)(2,1)}, u32[]{:S(2)}, u32[]{:S(2)}) collective-permute-start(bf16[6144,128]{1,0:T(8,128)(2,1)} %pack.1.refs_1_), channel_id=1, source_target_pairs={{0,8},{1,3},{2,10},{3,1},{4,12},{5,7},{6,14},{7,5},{8,16},{9,11},{... | collective-permute-start | bytes 4718600 | tf_op jit(solution)/shard_map/ppermute | solution.py:42
  46.3 0.0 collective-permute-done.refs_3_
  46.3 0.0 collective-permute-done.1.refs_4_
  46.3 0.0 all-to-all-done.refs_0_
  46.3 0.0 collective-permute-done.4.refs_7_
  46.3 0.0 collective-permute-done.5.refs_8_
  46.3 0.0 copy-done.1
  46.3 0.0 copy-start.2
  46.4 1.1 copy-done.2
  47.5 4.4 %ffn.2 = bf16[16,8,2048]{2,1,0:T(8,128)(2,1)} custom-call(bf16[16,8,2048]{2,1,0:T(8,128)(2,1)S(1)} %all-to-all-done.refs_0_, bf16[3072,128]{1,0:T(8,128)(2,1)S(1)} %copy-done.1, bf16[3072,128]{1,0:T(8,128)(2,1)S(1)} %copy-done.2, bf16[3072,128]{1,0:T(8,128)(2,1)} %collective-permute-done.refs_3_, bf16[3072,128]{1,0:T(8,128)(2,1)} %collective-permute-done.1.refs_4_, ...), custom_call_target="tpu_custom_call" | custom-call | flops 805306368 | bytes 6291456 | tf_op jit(solution)/shard_map/ffn/pallas_call | solution.py:256
  51.9 0.0 copy-start.4
  51.9 0.0 copy-start.5
  51.9 6.0 %all-to-all-start.1 = ((bf16[16,8,2048]{2,1,0:T(8,128)(2,1)}), bf16[16,8,2048]{2,1,0:T(8,128)(2,1)S(1)}, u32[]{:S(2)}, u32[]{:S(2)}) async-start(bf16[16,8,2048]{2,1,0:T(8,128)(2,1)} %ffn.2), calls=%async_computation.1 | async-start | bytes 1048576 | tf_op jit(solution)/shard_map/all_to_all | solution.py:46
  57.9 0.0 copy-done
  57.9 1.9 %collective-permute-start.7 = (bf16[6144,128]{1,0:T(8,128)(2,1)S(1)}, bf16[6144,128]{1,0:T(8,128)(2,1)}, u32[]{:S(2)}, u32[]{:S(2)}) collective-permute-start(bf16[6144,128]{1,0:T(8,128)(2,1)S(1)} %copy-done), channel_id=1, source_target_pairs={{0,1},{1,0},{2,3},{3,2},{4,5},{5,4},{6,7},{7,6},{8,9},{9,8},{10,11... | collective-permute-start | bytes 4718600 | tf_op jit(solution)/shard_map/ppermute | solution.py:36
  59.8 17.0 %collective-permute-done.8.refs_3_ = bf16[6144,128]{1,0:T(8,128)(2,1)} collective-permute-done((bf16[6144,128]{1,0:T(8,128)(2,1)}, bf16[6144,128]{1,0:T(8,128)(2,1)}, u32[]{:S(2)}, u32[]{:S(2)}) %collective-permute-start.8) | collective-permute-done | bytes 1572896 | tf_op jit(solution)/shard_map/ppermute | solution.py:42
  76.8 1.9 %collective-permute-start.9 = (bf16[6144,128]{1,0:T(8,128)(2,1)}, bf16[6144,128]{1,0:T(8,128)(2,1)}, u32[]{:S(2)}, u32[]{:S(2)}) collective-permute-start(bf16[6144,128]{1,0:T(8,128)(2,1)} %collective-permute-done.8.refs_3_), channel_id=1, source_target_pairs={{0,1},{1,0},{2,3},{3,2},{4,5},{5,4},{6,7},{7,6},{8,9},{9,8},{10,11... | collective-permute-start | bytes 4718600 | tf_op jit(solution)/shard_map/ppermute | solution.py:36
  78.7 2.0 %all-to-all-done.1.parts_ref = bf16[16,8,2048]{2,1,0:T(8,128)(2,1)S(1)} async-done(((bf16[16,8,2048]{2,1,0:T(8,128)(2,1)}), bf16[16,8,2048]{2,1,0:T(8,128)(2,1)S(1)}, u32[]{:S(2)}, u32[]{:S(2)}) %all-to-all-start.1) | async-done | bytes 524320 | tf_op jit(solution)/shard_map/all_to_all | solution.py:46
  80.7 0.0 copy-done.3
  80.7 0.1 advance.2
  80.8 5.3 %collective-permute-start.6 = (bf16[8,2048]{1,0:T(8,128)(2,1)S(1)}, bf16[8,2048]{1,0:T(8,128)(2,1)S(1)}, u32[]{:S(2)}, u32[]{:S(2)}) collective-permute-start(bf16[8,2048]{1,0:T(8,128)(2,1)S(1)} %advance.2), channel_id=1, source_target_pairs={{704,0},{0,64},{64,128},{128,192},{192,256},{256,320},{320,384},{3... | collective-permute-start | bytes 98312 | tf_op jit(solution)/shard_map/ppermute | solution.py:19
  86.0 7.0 %collective-permute-done.6.refs_1_.rows_ref = bf16[8,2048]{1,0:T(8,128)(2,1)S(1)} collective-permute-done((bf16[8,2048]{1,0:T(8,128)(2,1)S(1)}, bf16[8,2048]{1,0:T(8,128)(2,1)S(1)}, u32[]{:S(2)}, u32[]{:S(2)}) %collective-permute-start.6) | collective-permute-done | bytes 32800 | tf_op jit(solution)/shard_map/ppermute | solution.py:19
  93.0 0.0 copy-done.4
  93.0 1.5 spread.1
  94.5 8.9 %all-to-all-start.2 = ((bf16[16,8,2048]{2,1,0:T(8,128)(2,1)}), bf16[16,8,2048]{2,1,0:T(8,128)(2,1)S(1)}, u32[]{:S(2)}, u32[]{:S(2)}) async-start(bf16[16,8,2048]{2,1,0:T(8,128)(2,1)} %spread.1), calls=%async_computation.2 | async-start | bytes 1048576 | tf_op jit(solution)/shard_map/all_to_all | solution.py:46
  103.4 0.0 collective-permute-done.7.refs_2_
  103.4 0.0 collective-permute-done.9.refs_4_
  103.4 17.1 %all-to-all-done.2.refs_0_ = bf16[16,8,2048]{2,1,0:T(8,128)(2,1)S(1)} async-done(((bf16[16,8,2048]{2,1,0:T(8,128)(2,1)}), bf16[16,8,2048]{2,1,0:T(8,128)(2,1)S(1)}, u32[]{:S(2)}, u32[]{:S(2)}) %all-to-all-start.2) | async-done | bytes 524320 | tf_op jit(solution)/shard_map/all_to_all | solution.py:46
  120.5 3.4 %ffn.3 = bf16[16,8,2048]{2,1,0:T(8,128)(2,1)S(1)} custom-call(bf16[16,8,2048]{2,1,0:T(8,128)(2,1)S(1)} %all-to-all-done.2.refs_0_, bf16[6144,128]{1,0:T(8,128)(2,1)S(1)} %copy-done, bf16[6144,128]{1,0:T(8,128)(2,1)} %collective-permute-done.7.refs_2_, bf16[6144,128]{1,0:T(8,128)(2,1)} %collective-permute-done.8.refs_3_, ...), custom_call_target="tpu_custom_call" | custom-call | flops 805306368 | bytes 6291456 | tf_op jit(solution)/shard_map/ffn/pallas_call | solution.py:256
  124.0 21.7 %all_to_all.20.parts_ref = bf16[16,8,2048]{2,1,0:T(8,128)(2,1)S(1)} all-to-all(bf16[16,8,2048]{2,1,0:T(8,128)(2,1)S(1)} %ffn.3), channel_id=1, replica_groups={{0,16,32,48,10,26,42,58,4,20,36,52,14,30,46,62},{8,24,40,56,2,18,34,50,..., dimensions={0} | all-to-all | bytes 1048576 | tf_op jit(solution)/shard_map/all_to_all | solution.py:46
  145.7 0.1 advance.3
  145.8 3.0 %collective-permute-start.10 = (bf16[8,2048]{1,0:T(8,128)(2,1)S(1)}, bf16[8,2048]{1,0:T(8,128)(2,1)S(1)}, u32[]{:S(2)}, u32[]{:S(2)}) collective-permute-start(bf16[8,2048]{1,0:T(8,128)(2,1)S(1)} %advance.3), channel_id=1, source_target_pairs={{704,0},{0,64},{64,128},{128,192},{192,256},{256,320},{320,384},{3... | collective-permute-start | bytes 98312 | tf_op jit(solution)/shard_map/ppermute | solution.py:19
  148.8 9.4 %collective-permute-done.10 = bf16[8,2048]{1,0:T(8,128)(2,1)S(1)} collective-permute-done((bf16[8,2048]{1,0:T(8,128)(2,1)S(1)}, bf16[8,2048]{1,0:T(8,128)(2,1)S(1)}, u32[]{:S(2)}, u32[]{:S(2)}) %collective-permute-start.10) | collective-permute-done | bytes 32800 | tf_op jit(solution)/shard_map/ppermute | solution.py:19
  158.2 0.6 copy.8
  (1 shorter events, 0.0 us)
Async XLA Ops:
  3.9 31.0 %collective-permute-start.2 = (bf16[3072,128]{1,0:T(8,128)(2,1)}, bf16[3072,128]{1,0:T(8,128)(2,1)}, u32[]{:S(2)}, u32[]{:S(2)}) collective-permute-start(bf16[3072,128]{1,0:T(8,128)(2,1)} %get-tuple-element.9.refs_1_), channel_id=1, source_target_pairs={{0,56},{1,3},{2,58},{3,1},{4,60},{5,7},{6,62},{7,5},{8,0},{9,11},{... | collective-permute-start | bytes 2359304 | tf_op jit(solution)/shard_map/ppermute | solution.py:42
  15.2 23.7 %collective-permute-start.3 = (bf16[3072,128]{1,0:T(8,128)(2,1)}, bf16[3072,128]{1,0:T(8,128)(2,1)}, u32[]{:S(2)}, u32[]{:S(2)}) collective-permute-start(bf16[3072,128]{1,0:T(8,128)(2,1)} %get-tuple-element.10.refs_2_), channel_id=1, source_target_pairs={{0,8},{1,3},{2,10},{3,1},{4,12},{5,7},{6,14},{7,5},{8,16},{9,11},{... | collective-permute-start | bytes 2359304 | tf_op jit(solution)/shard_map/ppermute | solution.py:42
  17.2 29.1 %all-to-all-start = ((bf16[16,8,2048]{2,1,0:T(8,128)(2,1)}), bf16[16,8,2048]{2,1,0:T(8,128)(2,1)S(1)}, u32[]{:S(2)}, u32[]{:S(2)}) async-start(bf16[16,8,2048]{2,1,0:T(8,128)(2,1)} %get-tuple-element.8), calls=%async_computation | async-start | bytes 1048576 | tf_op jit(solution)/shard_map/all_to_all | solution.py:46
  21.4 25.0 %copy-start.1 = (bf16[3072,128]{1,0:T(8,128)(2,1)S(1)}, bf16[3072,128]{1,0:T(8,128)(2,1)}, u32[]{:S(2)}) copy-start(bf16[3072,128]{1,0:T(8,128)(2,1)} %get-tuple-element.9.refs_1_) | copy-start | bytes 2359300
  21.4 24.9 %collective-permute-start = (bf16[3072,128]{1,0:T(8,128)(2,1)}, bf16[3072,128]{1,0:T(8,128)(2,1)}, u32[]{:S(2)}, u32[]{:S(2)}) collective-permute-start(bf16[3072,128]{1,0:T(8,128)(2,1)} %get-tuple-element.9.refs_1_), channel_id=1, source_target_pairs={{0,1},{1,0},{2,3},{3,2},{4,5},{5,4},{6,7},{7,6},{8,9},{9,8},{10,11... | collective-permute-start | bytes 2359304 | tf_op jit(solution)/shard_map/ppermute | solution.py:36
  23.5 22.8 %collective-permute-start.1 = (bf16[3072,128]{1,0:T(8,128)(2,1)}, bf16[3072,128]{1,0:T(8,128)(2,1)}, u32[]{:S(2)}, u32[]{:S(2)}) collective-permute-start(bf16[3072,128]{1,0:T(8,128)(2,1)} %get-tuple-element.10.refs_2_), channel_id=1, source_target_pairs={{0,1},{1,0},{2,3},{3,2},{4,5},{5,4},{6,7},{7,6},{8,9},{9,8},{10,11... | collective-permute-start | bytes 2359304 | tf_op jit(solution)/shard_map/ppermute | solution.py:36
  34.9 11.4 %collective-permute-start.4 = (bf16[3072,128]{1,0:T(8,128)(2,1)}, bf16[3072,128]{1,0:T(8,128)(2,1)}, u32[]{:S(2)}, u32[]{:S(2)}) collective-permute-start(bf16[3072,128]{1,0:T(8,128)(2,1)} %collective-permute-done.2.refs_5_), channel_id=1, source_target_pairs={{0,1},{1,0},{2,3},{3,2},{4,5},{5,4},{6,7},{7,6},{8,9},{9,8},{10,11... | collective-permute-start | bytes 2359304 | tf_op jit(solution)/shard_map/ppermute | solution.py:36
  38.9 7.4 %collective-permute-start.5 = (bf16[3072,128]{1,0:T(8,128)(2,1)}, bf16[3072,128]{1,0:T(8,128)(2,1)}, u32[]{:S(2)}, u32[]{:S(2)}) collective-permute-start(bf16[3072,128]{1,0:T(8,128)(2,1)} %collective-permute-done.3.refs_6_), channel_id=1, source_target_pairs={{0,1},{1,0},{2,3},{3,2},{4,5},{5,4},{6,7},{7,6},{8,9},{9,8},{10,11... | collective-permute-start | bytes 2359304 | tf_op jit(solution)/shard_map/ppermute | solution.py:36
  40.8 39.9 %copy-start.3 = (bf16[1,8,2048]{2,1,0:T(8,128)(2,1)S(1)}, bf16[1,8,2048]{2,1,0:T(8,128)(2,1)}, u32[]{:S(2)}) copy-start(bf16[1,8,2048]{2,1,0:T(8,128)(2,1)} %param.6) | copy-start | bytes 98308
  44.2 13.7 %copy-start = (bf16[6144,128]{1,0:T(8,128)(2,1)S(1)}, bf16[6144,128]{1,0:T(8,128)(2,1)}, u32[]{:S(2)}) copy-start(bf16[6144,128]{1,0:T(8,128)(2,1)} %pack.1.refs_1_) | copy-start | bytes 4718596
  44.2 32.6 %collective-permute-start.8 = (bf16[6144,128]{1,0:T(8,128)(2,1)}, bf16[6144,128]{1,0:T(8,128)(2,1)}, u32[]{:S(2)}, u32[]{:S(2)}) collective-permute-start(bf16[6144,128]{1,0:T(8,128)(2,1)} %pack.1.refs_1_), channel_id=1, source_target_pairs={{0,8},{1,3},{2,10},{3,1},{4,12},{5,7},{6,14},{7,5},{8,16},{9,11},{... | collective-permute-start | bytes 4718600 | tf_op jit(solution)/shard_map/ppermute | solution.py:42
  46.3 1.1 copy-start.2
  51.9 41.1 %copy-start.4 = (f32[1,2,2048]{2,1,0:T(2,128)S(1)}, f32[1,2,2048]{2,1,0:T(2,128)}, u32[]{:S(2)}) copy-start(f32[1,2,2048]{2,1,0:T(2,128)} %param.10) | copy-start | bytes 49156
  51.9 41.1 %copy-start.5 = (s32[2,1]{0,1:T(1,128)S(1)}, s32[2,1]{0,1:T(1,128)}, u32[]{:S(2)}) copy-start(s32[2,1]{0,1:T(1,128)} %param.11) | copy-start | bytes 28
  51.9 28.8 %all-to-all-start.1 = ((bf16[16,8,2048]{2,1,0:T(8,128)(2,1)}), bf16[16,8,2048]{2,1,0:T(8,128)(2,1)S(1)}, u32[]{:S(2)}, u32[]{:S(2)}) async-start(bf16[16,8,2048]{2,1,0:T(8,128)(2,1)} %ffn.2), calls=%async_computation.1 | async-start | bytes 1048576 | tf_op jit(solution)/shard_map/all_to_all | solution.py:46
  57.9 45.5 %collective-permute-start.7 = (bf16[6144,128]{1,0:T(8,128)(2,1)S(1)}, bf16[6144,128]{1,0:T(8,128)(2,1)}, u32[]{:S(2)}, u32[]{:S(2)}) collective-permute-start(bf16[6144,128]{1,0:T(8,128)(2,1)S(1)} %copy-done), channel_id=1, source_target_pairs={{0,1},{1,0},{2,3},{3,2},{4,5},{5,4},{6,7},{7,6},{8,9},{9,8},{10,11... | collective-permute-start | bytes 4718600 | tf_op jit(solution)/shard_map/ppermute | solution.py:36
  76.8 26.6 %collective-permute-start.9 = (bf16[6144,128]{1,0:T(8,128)(2,1)}, bf16[6144,128]{1,0:T(8,128)(2,1)}, u32[]{:S(2)}, u32[]{:S(2)}) collective-permute-start(bf16[6144,128]{1,0:T(8,128)(2,1)} %collective-permute-done.8.refs_3_), channel_id=1, source_target_pairs={{0,1},{1,0},{2,3},{3,2},{4,5},{5,4},{6,7},{7,6},{8,9},{9,8},{10,11... | collective-permute-start | bytes 4718600 | tf_op jit(solution)/shard_map/ppermute | solution.py:36
  80.8 12.3 %collective-permute-start.6 = (bf16[8,2048]{1,0:T(8,128)(2,1)S(1)}, bf16[8,2048]{1,0:T(8,128)(2,1)S(1)}, u32[]{:S(2)}, u32[]{:S(2)}) collective-permute-start(bf16[8,2048]{1,0:T(8,128)(2,1)S(1)} %advance.2), channel_id=1, source_target_pairs={{704,0},{0,64},{64,128},{128,192},{192,256},{256,320},{320,384},{3... | collective-permute-start | bytes 98312 | tf_op jit(solution)/shard_map/ppermute | solution.py:19
  94.5 26.0 %all-to-all-start.2 = ((bf16[16,8,2048]{2,1,0:T(8,128)(2,1)}), bf16[16,8,2048]{2,1,0:T(8,128)(2,1)S(1)}, u32[]{:S(2)}, u32[]{:S(2)}) async-start(bf16[16,8,2048]{2,1,0:T(8,128)(2,1)} %spread.1), calls=%async_computation.2 | async-start | bytes 1048576 | tf_op jit(solution)/shard_map/all_to_all | solution.py:46
  145.8 12.5 %collective-permute-start.10 = (bf16[8,2048]{1,0:T(8,128)(2,1)S(1)}, bf16[8,2048]{1,0:T(8,128)(2,1)S(1)}, u32[]{:S(2)}, u32[]{:S(2)}) collective-permute-start(bf16[8,2048]{1,0:T(8,128)(2,1)S(1)} %advance.3), channel_id=1, source_target_pairs={{704,0},{0,64},{64,128},{128,192},{192,256},{256,320},{320,384},{3... | collective-permute-start | bytes 98312 | tf_op jit(solution)/shard_map/ppermute | solution.py:19
